TPU v7x, 1024 devices: a whole 8x8x8 slice. The times are simulated.
1024 devices in a mesh: win: 64 (over y, z_hi, core), seq: 16 (over x, z_lo).
Axes of the slice: x: 8, y: 8, z: 8 (z_hi: 4, z_lo: 2; z = z_hi * 2 + z_lo), core: 2. Of those that a mesh axis runs over, the one named last changes fastest.
Arguments:
- qkv_grid: bfloat16 [90, 64, 32, 4608], P(None, 'win', 'seq'), may hold values from -160 to 160
- tokens: bfloat16 [90, 64, 32, 1536], P(None, 'win', 'seq'), may hold values from -6 to 6
- out_weight: bfloat16 [1536, 1536], replicated, may hold values from -0.625 to 0.625
- regions: int32 [90, 64, 32], P(None, 'win'), may hold values from 0 to 2, as said below
Outputs:
- mixed: bfloat16 [90, 64, 32, 1536], P(None, 'win', 'seq')
Inputs may be any that keep to these rules, and one draw needn't show every extreme that they name: `regions`: columns 2m and 2m+1 of a window always have the same region id.
All inputs are finite; a program needn't handle non-finite values.
Results may differ from a plain program's by a relative error of at most 0.01.
Values may be sent and summed in bfloat16 or wider, within the bound.
No kernel may reach another device: no remote copies, remote signals or barrier semaphores. Data moves between devices by JAX's collectives and lax.ppermute only.
A program may use at most 32 MiB of HBM per device.

v0:
```python
import jax
import jax.numpy as jnp
from jax import lax
from jax.sharding import PartitionSpec as P

D = 1536
HEADS = 16
HD = 96
WH = 30
WW = 32


def from_behind(block, axis, distance):
    devices = range(lax.axis_size(axis))
    route = [((i - distance) % len(devices), i) for i in devices]
    return lax.ppermute(block, axis, route)


def attend(window_block, labels):
    queries = window_block[:, 0]
    key_rows = window_block[:, 1]
    values = window_block[:, 2]
    scores = jnp.einsum(
        "qhd,khd->hqk", queries, key_rows, preferred_element_type=jnp.float32
    ) * HD ** (-0.5)
    allowed = labels[:, None] == labels[None, :]
    scores = jnp.where(allowed[None], scores, -1e30)
    largest = jnp.max(scores, axis=-1, keepdims=True)
    weights = jnp.exp(scores - largest)
    soft_weights = (weights / jnp.sum(weights, axis=-1, keepdims=True)).astype(jnp.bfloat16)
    result = jnp.einsum("hqk,khd->qhd", soft_weights, values, preferred_element_type=jnp.float32)
    return result.astype(jnp.bfloat16)


def one_window(paired):
    return attend(paired[0], paired[1])


def window_attention(flat_grid, labels_flat):
    row_total, col_total, three, heads_here, head_size = flat_grid.shape
    bands = row_total // WH
    window_count = col_total // WW
    blocks = flat_grid.reshape(bands, WH, window_count, WW, three, heads_here, head_size)
    blocks = blocks.transpose(0, 2, 1, 3, 4, 5, 6).reshape(
        bands * window_count, WH * WW, three, heads_here, head_size
    )
    labels = (
        labels_flat.reshape(bands, WH, window_count, WW)
        .transpose(0, 2, 1, 3)
        .reshape(bands * window_count, WH * WW)
    )
    attended = lax.map(one_window, (blocks, labels))
    attended = attended.reshape(bands, window_count, WH, WW, heads_here, head_size).transpose(
        0, 2, 1, 3, 4, 5
    )
    return attended.reshape(row_total, col_total, heads_here, head_size)


def per_device(qkv_grid, tokens, out_weight, regions):
    seq_count = lax.axis_size("seq")
    lat_rows, win_count, col_count, packed_width = qkv_grid.shape
    labels_local = regions.reshape(lat_rows, win_count * WW)
    half_cols = WW // 2
    half_rows = WH // 2
    group_heads = HEADS // seq_count
    split_heads = qkv_grid.reshape(lat_rows, win_count, col_count, 3, seq_count, group_heads, HD)
    gathered = lax.all_to_all(split_heads, "seq", split_axis=4, concat_axis=2, tiled=True)
    flat_grid = gathered.reshape(lat_rows, win_count * WW, 3, group_heads, HD)
    arriving = from_behind(flat_grid[:, :half_cols], "win", -1)
    shifted = jnp.concatenate([flat_grid[:, half_cols:], arriving], axis=1)
    shifted = jnp.roll(shifted, -half_rows, axis=0)
    result = window_attention(shifted, labels_local)
    result = jnp.roll(result, half_rows, axis=0)
    leaving = from_behind(result[:, -half_cols:], "win", 1)
    result = jnp.concatenate([leaving, result[:, :-half_cols]], axis=1)
    attended = result.reshape(lat_rows, win_count, WW, 1, group_heads, HD)
    returned = lax.all_to_all(attended, "seq", split_axis=2, concat_axis=3, tiled=True)
    mixed_in = returned.reshape(lat_rows, win_count, col_count, D)
    projected = jnp.dot(mixed_in.reshape(-1, D), out_weight, preferred_element_type=jnp.float32)
    total = projected + tokens.reshape(-1, D).astype(jnp.float32)
    return total.astype(jnp.bfloat16).reshape(tokens.shape)


def solution(mesh):
    in_specs = (P(None, "win", "seq", None), P(None, "win", "seq", None), P(), P(None, "win", None))
    out_specs = P(None, "win", "seq", None)
    return jax.shard_map(
        per_device, mesh=mesh, in_specs=in_specs, out_specs=out_specs, check_vma=False
    )
```

profile of v0, /device:TPU:112, one launch (start us, length us, event | category | flops | bytes accessed | tf_op | source)
XLA Modules:
  0.0 173.9 jit_solution(7376035889624997229)
XLA Ops:
  0.0 4.5 %reshape.52 = bf16[90,1,2,3,16,1,96]{6,4,3,2,0,5,1:T(8,128)(2,1)S(1)} reshape(bf16[90,1,2,4608]{3,2,1,0:T(2,128)(2,1)} %param.6) | data formatting | bytes 3317760 | tf_op jit(solution)/shard_map/reshape | solution.py:66
  4.5 1.7 copy.29
  6.2 63.6 %all_to_all.30 = bf16[90,1,2,3,16,1,96]{6,2,5,3,1,0,4:T(2,128)(2,1)S(1)} all-to-all(bf16[90,1,2,3,16,1,96]{6,2,5,3,1,0,4:T(2,128)(2,1)S(1)} %copy.29), channel_id=1, replica_groups=mesh['win'=64,'seq'=16] {'seq'}, dimensions={4} | all-to-all | bytes 3317760 | tf_op jit(solution)/shard_map/all_to_all | solution.py:67
  69.9 0.0 copy-start.2
  69.9 1.5 copy.30
  71.4 0.4 fusion.15
  71.8 14.2 %collective-permute-start = (bf16[90,16,3,1,96]{4,1,2,0,3:T(8,128)(2,1)S(1)}, bf16[90,16,3,1,96]{4,1,2,0,3:T(8,128)(2,1)S(1)}, u32[]{:S(2)}, u32[]{:S(2)}) collective-permute-start(bf16[90,16,3,1,96]{4,1,2,0,3:T(8,128)(2,1)S(1)} %get-tuple-element.55), channel_id=1, source_target_pairs={{16,0},{32,16},{48,32},{64,48},{80,64},{96,80},{112,96},{128,112},... | collective-permute-start | bytes 2488328 | tf_op jit(solution)/shard_map/ppermute | solution.py:16
  86.0 0.0 copy-done.2
  86.0 0.1 copy.32
  86.1 0.1 reshape_transpose_reshape_reshape.3
  86.2 24.3 %collective-permute-done = bf16[90,16,3,1,96]{4,1,2,0,3:T(8,128)(2,1)S(1)} collective-permute-done((bf16[90,16,3,1,96]{4,1,2,0,3:T(8,128)(2,1)S(1)}, bf16[90,16,3,1,96]{4,1,2,0,3:T(8,128)(2,1)S(1)}, u32[]{:S(2)}, u32[]{:S(2)}) %collective-permute-start) | collective-permute-done | bytes 829472 | tf_op jit(solution)/shard_map/ppermute | solution.py:16
  110.5 0.4 fusion.11
  110.9 0.4 fusion.10
  111.3 0.0 copy-start
  111.4 1.7 %copy.31 = bf16[90,32,3,1,96]{4,1,0,2,3:T(8,128)(2,1)} copy(bf16[90,32,3,1,96]{4,1,2,0,3:T(8,128)(2,1)S(1)} %fusion.10) | data formatting | bytes 3317760 | tf_op jit(solution)/shard_map/jit(_roll_static)/concatenate | solution.py:71
  113.1 2.8 %copy.33 = bf16[3,960,3,1,96]{1,4,3,2,0:T(8,128)(2,1)S(1)} copy(bf16[3,960,3,1,96]{4,1,0,2,3:T(8,128)(2,1)} %bitcast.59) | data formatting | bytes 3317760 | tf_op jit(solution)/shard_map/while | solution.py:52
  115.9 0.0 copy-done
  115.9 9.6 %while.10 = (s32[]{:T(128)}, bf16[3,960,1,96]{1,3,2,0:T(8,128)(2,1)S(1)}, bf16[3,960,3,1,96]{1,4,3,2,0:T(8,128)(2,1)S(1)}, s32[3,960]{1,0:T(4,128)S(1)}, s32[]{:T(128)}) while((s32[]{:T(128)}, bf16[3,960,1,96]{1,3,2,0:T(8,128)(2,1)S(1)}, bf16[3,960,3,1,96]{1,4,3,2,0:T(8,128)(2,1)S(1)}, s32[3,960]{1,0:T(4,128)S(1)}, s32[]{:T(128)}) %tuple.29), condition=%wide.region_3.4_spmd, body=%wide.region_0.3_spmd.sunk | while | flops 367808640 | bytes 13245001 | solution.py:52
  116.0 0.8 fusion.21
  116.8 1.0 fusion.22
  117.8 1.3 fusion.23
  119.2 0.8 fusion.21
  120.1 1.0 fusion.22
  121.0 1.3 fusion.23
  122.4 0.8 fusion.21
  123.3 1.0 fusion.22
  124.3 1.3 fusion.23
  125.5 0.4 copy.34
  125.9 0.0 copy-start.1
  126.0 0.1 fusion.14
  126.1 5.5 %collective-permute-start.1 = (bf16[90,16,1,96]{3,1,0,2:T(8,128)(2,1)S(1)}, bf16[90,16,1,96]{3,1,0,2:T(8,128)(2,1)S(1)}, u32[]{:S(2)}, u32[]{:S(2)}) collective-permute-start(bf16[90,16,1,96]{3,1,0,2:T(8,128)(2,1)S(1)} %fusion.14), channel_id=1, source_target_pairs={{1008,0},{0,16},{16,32},{32,48},{48,64},{64,80},{80,96},{96,112},{... | collective-permute-start | bytes 829448 | tf_op jit(solution)/shard_map/ppermute | solution.py:16
  131.6 8.6 %collective-permute-done.1 = bf16[90,16,1,96]{3,1,0,2:T(8,128)(2,1)S(1)} collective-permute-done((bf16[90,16,1,96]{3,1,0,2:T(8,128)(2,1)S(1)}, bf16[90,16,1,96]{3,1,0,2:T(8,128)(2,1)S(1)}, u32[]{:S(2)}, u32[]{:S(2)}) %collective-permute-start.1) | collective-permute-done | bytes 276512 | tf_op jit(solution)/shard_map/ppermute | solution.py:16
  140.2 0.1 fusion.13
  140.3 1.2 copy.35
  141.5 3.9 %all-to-all-start.1 = ((bf16[90,1,32,1,1,96]{5,0,4,3,1,2:T(8,128)(2,1)}), bf16[90,1,32,1,1,96]{5,0,4,3,1,2:T(8,128)(2,1)S(1)}, u32[]{:S(2)}, u32[]{:S(2)}) async-start(bf16[90,1,32,1,1,96]{5,0,4,3,1,2:T(8,128)(2,1)} %copy.35), calls=%async_computation.1 | async-start | bytes 1572864 | tf_op jit(solution)/shard_map/all_to_all | solution.py:77
  145.4 0.0 copy-done.1
  145.4 0.2 reshape.56
  145.5 22.5 %all-to-all-done.1 = bf16[90,1,32,1,1,96]{5,0,4,3,1,2:T(8,128)(2,1)S(1)} async-done(((bf16[90,1,32,1,1,96]{5,0,4,3,1,2:T(8,128)(2,1)}), bf16[90,1,32,1,1,96]{5,0,4,3,1,2:T(8,128)(2,1)S(1)}, u32[]{:S(2)}, u32[]{:S(2)}) %all-to-all-start.1) | async-done | bytes 552992 | tf_op jit(solution)/shard_map/all_to_all | solution.py:77
  168.0 0.5 copy.39
  168.5 0.8 reshape_reshape.3
  169.3 3.4 %fusion.9 = bf16[180,1536]{1,0:T(8,128)(2,1)S(1)} fusion(f32[180,1536]{1,0:T(8,128)S(1)} %reshape.56, bf16[180,1536]{1,0:T(8,128)(2,1)S(1)} %reshape_reshape.3, bf16[1536,1536]{1,0:T(8,128)(2,1)} %param.8), kind=kOutput, calls=%fused_computation.18 | convolution fusion | flops 849899520 | bytes 6930432 | tf_op jit(solution)/shard_map/dot_general | solution.py:79
  172.7 1.2 reshape.55
  (9 shorter events, 0.2 us)
Async XLA Ops:
  69.9 16.1 %copy-start.2 = (s32[90,1,32]{0,2,1:T(8,128)S(1)}, s32[90,1,32]{0,2,1:T(8,128)}, u32[]{:S(2)}) copy-start(s32[90,1,32]{0,2,1:T(8,128)} %param.9) | copy-start | bytes 34564
  71.8 38.8 %collective-permute-start = (bf16[90,16,3,1,96]{4,1,2,0,3:T(8,128)(2,1)S(1)}, bf16[90,16,3,1,96]{4,1,2,0,3:T(8,128)(2,1)S(1)}, u32[]{:S(2)}, u32[]{:S(2)}) collective-permute-start(bf16[90,16,3,1,96]{4,1,2,0,3:T(8,128)(2,1)S(1)} %get-tuple-element.55), channel_id=1, source_target_pairs={{16,0},{32,16},{48,32},{64,48},{80,64},{96,80},{112,96},{128,112},... | collective-permute-start | bytes 2488328 | tf_op jit(solution)/shard_map/ppermute | solution.py:16
  111.3 4.6 %copy-start = (bf16[3,960,1,96]{1,3,2,0:T(8,128)(2,1)S(1)}, bf16[3,960,1,96]{1,3,2,0:T(8,128)(2,1)}, u32[]{:S(2)}) copy-start(bf16[3,960,1,96]{1,3,2,0:T(8,128)(2,1)} %custom-call) | copy-start | bytes 1658884
  125.9 19.4 %copy-start.1 = (bf16[90,1,2,1536]{3,2,1,0:T(2,128)(2,1)S(1)}, bf16[90,1,2,1536]{3,2,1,0:T(2,128)(2,1)}, u32[]{:S(2)}) copy-start(bf16[90,1,2,1536]{3,2,1,0:T(2,128)(2,1)} %param.7) | copy-start | bytes 1658884
  126.1 14.1 %collective-permute-start.1 = (bf16[90,16,1,96]{3,1,0,2:T(8,128)(2,1)S(1)}, bf16[90,16,1,96]{3,1,0,2:T(8,128)(2,1)S(1)}, u32[]{:S(2)}, u32[]{:S(2)}) collective-permute-start(bf16[90,16,1,96]{3,1,0,2:T(8,128)(2,1)S(1)} %fusion.14), channel_id=1, source_target_pairs={{1008,0},{0,16},{16,32},{32,48},{48,64},{64,80},{80,96},{96,112},{... | collective-permute-start | bytes 829448 | tf_op jit(solution)/shard_map/ppermute | solution.py:16
  141.5 26.5 %all-to-all-start.1 = ((bf16[90,1,32,1,1,96]{5,0,4,3,1,2:T(8,128)(2,1)}), bf16[90,1,32,1,1,96]{5,0,4,3,1,2:T(8,128)(2,1)S(1)}, u32[]{:S(2)}, u32[]{:S(2)}) async-start(bf16[90,1,32,1,1,96]{5,0,4,3,1,2:T(8,128)(2,1)} %copy.35), calls=%async_computation.1 | async-start | bytes 1572864 | tf_op jit(solution)/shard_map/all_to_all | solution.py:77
where the time goes:
time: 174 us
  blocking collectives  63.6 us (37%)
  waiting for transfers between devices  55.4 us (32%)
  starting transfers between devices  23.6 us (14%)
  local copies, waits for them, and re-layouts  17.3 us (10%)
  matrix products  9.73 us (6%)
  other arithmetic  3.98 us (2%)
    all_to_all x1, blocking collectives, per_device(): lax.all_to_all(split_heads, 'seq', split_axis=4, concat_axis=2, tiled=True)  63.6 us
    ppermute x2, waiting for transfers between devices, from_behind(): return lax.ppermute(block, axis, route)  32.9 us
    all_to_all x1, waiting for transfers between devices, per_device(): lax.all_to_all(attended, 'seq', split_axis=2, concat_axis=3, tiled=True)  22.5 us
    ppermute x2, starting transfers between devices, from_behind(): return lax.ppermute(block, axis, route)  19.7 us
    reshape x2, local copies, waits for them, and re-layouts, per_device(): qkv_grid.reshape(lat_rows, win_count, col_count, 3, seq_count, group_head...  6.22 us
    all_to_all x1, starting transfers between devices, per_device(): lax.all_to_all(attended, 'seq', split_axis=2, concat_axis=3, tiled=True)  3.85 us
    dot_general x3, matrix products, attend(): jnp.einsum('hqk,khd->qhd', soft_weights, values, preferred_element_type=j...  3.82 us
  transfers between devices with their start and end apart: 3, of which 3 were waited for; matrix products, arithmetic and copies ran while one was open for 0% of the time, Pallas kernels for 0%

commit v1 on v0

v1 whole, which is shorter than its diff:
```python
import jax
import jax.numpy as jnp
from jax import lax
from jax.experimental import pallas as pl
from jax.experimental.pallas import tpu as pltpu
from jax.sharding import PartitionSpec as P

D = 1536
HEADS = 16
HD = 96
WH = 30
WW = 32
BANDS = 3
ROWS = 64
PACK = 144
PIECE = 48
KEYS = HEADS * ROWS
HIDE = -1e30


def lane_block(rows):
    return lax.broadcasted_iota(jnp.int32, (rows, 128), 1) // 32


def head_lanes(load, h):
    g, j = divmod(h, 4)
    if j == 0:
        return load(3 * g)
    if j == 3:
        return load(3 * g + 2)
    first, second = load(3 * g + j - 1), load(3 * g + j)
    block = lane_block(first.shape[0])
    return jnp.where(block < 3 - j, second, first)


def pack_rows(load, h):
    tail = head_lanes(lambda t: load(t, PACK, PIECE), h).astype(jnp.float32)
    out = []
    for i in range(3):
        rows = head_lanes(lambda t: load(t, PIECE * i, PIECE), h)
        moved = pltpu.roll(tail, 32 * (3 - i), 1).astype(jnp.bfloat16)
        out.append(jnp.where(lane_block(PIECE) == 3 - h % 4, moved, rows))
    return out


def pack_in_kernel(x_ref, o_ref, flat):
    for b in range(BANDS):
        flat[ROWS * (b + 1) - 4:ROWS * (b + 1), :] = jnp.zeros((4, 3 * D), jnp.bfloat16)
    for dst, src, count in SPANS:
        for r in range(0, count, 8):
            n = min(8, count - r)
            start = 2 * (dst + r)
            flat[start:start + 2 * n, :] = x_ref[src + r:src + r + n, 0].reshape(2 * n, 3 * D)
    for t in range(3):
        for h in range(HEADS):
            def load(tile, start, size):
                lanes = (12 * t + tile) * 128
                return flat[start:start + size, lanes:lanes + 128]
            for i, rows in enumerate(pack_rows(load, h)):
                start = PACK * t + PIECE * i
                o_ref[h, start:start + PIECE, :] = rows


SPANS = ((0, 15, 30), (32, 45, 30), (64, 75, 15), (79, 0, 15))


def pack_qkv(x):
    return pl.pallas_call(
        pack_in_kernel,
        out_shape=jax.ShapeDtypeStruct((HEADS, 3 * PACK, 128), jnp.bfloat16),
        in_specs=[pl.BlockSpec(memory_space=pltpu.VMEM)],
        out_specs=pl.BlockSpec(memory_space=pltpu.VMEM),
        scratch_shapes=[pltpu.VMEM((BANDS * ROWS, 3 * D), jnp.bfloat16)],
        cost_estimate=pl.CostEstimate(flops=10**7, bytes_accessed=4 * 10**6, transcendentals=0),
        name="pack_qkv",
    )(x)


def attend_kernel(head_ref, x_ref, labels_ref, o_ref, q_s, k_s, v_s, r_s):
    junk = 3 - lax.rem(head_ref[0], 4)
    start = lax.rem(junk + 1, 4)
    f32, bf16 = jnp.float32, jnp.bfloat16
    scale = HD ** -0.5 * 1.4426950408889634

    def turned(x, shift):
        return pltpu.roll(x.astype(f32), shift, 1).astype(bf16)

    def tail_rows(rows):
        block = lane_block(PIECE)
        a, b, c = (turned(rows(i), 32 * (i + 1)) for i in range(3))
        second = lax.rem(start + 1, 4)
        return jnp.where(block == start, a, jnp.where(block == second, b, c))

    columns = labels_ref[...].astype(bf16)
    picks = (lax.broadcasted_iota(jnp.int32, (WW, HEADS * 128), 0)
             == 2 * (lax.broadcasted_iota(jnp.int32, (WW, HEADS * 128), 1) // 128))
    picks = picks.astype(bf16)
    lane = lax.broadcasted_iota(jnp.int32, (ROWS, 128), 1)
    region = lane - 32 * junk
    inside = (region >= 0) & (region < 32)
    for b in range(BANDS):
        token = lax.broadcasted_iota(jnp.int32, (ROWS, 90), 0)
        grows = (token // 2 + WH * b == lax.broadcasted_iota(jnp.int32, (ROWS, 90), 1)) & (token < 60)
        by_column = lax.dot_general(
            grows.astype(bf16), columns, (((1,), (1,)), ((), ())), preferred_element_type=f32)
        r_s[...] = jnp.dot(by_column.astype(bf16), picks, preferred_element_type=f32)
        pad = lax.broadcasted_iota(jnp.int32, (ROWS, 128), 0) >= 60
        for p in range(HEADS):
            label = jnp.where(pad, 3, r_s[:, 128 * p:128 * (p + 1)].astype(jnp.int32))
            same = label == region
            rows = []
            for t in range(3):
                if b < 2:
                    rows.append(x_ref[p, PACK * t + ROWS * b:PACK * t + ROWS * (b + 1), :])
                else:
                    head = x_ref[p, PACK * t + 2 * ROWS:PACK * (t + 1), :]
                    tail = tail_rows(lambda i: x_ref[p, PACK * t + PIECE * i:PACK * t + PIECE * (i + 1), :])
                    rows.append(jnp.concatenate([head, tail], 0))
            here = slice(ROWS * p, ROWS * (p + 1))
            q_s[here, :] = jnp.where(inside, jnp.where(same, 1.0, 0.0).astype(bf16), rows[0])
            k_s[here, :] = jnp.where(inside, jnp.where(same, 0.0, HIDE).astype(bf16), rows[1])
            v_s[here, :128] = rows[2]
        v_s[:, 128:] = jnp.ones((KEYS, 128), bf16)
        block_rows = 256
        for n in range(KEYS // block_rows):
            q = q_s[block_rows * n:block_rows * (n + 1), :]
            s = lax.dot_general(q, k_s[...], (((1,), (1,)), ((), ())), preferred_element_type=f32)
            m = jnp.max(s, axis=1, keepdims=True)
            weights = jnp.exp2((s - m) * scale).astype(bf16)
            acc = jnp.dot(weights, v_s[...], preferred_element_type=f32)
            out = (acc[:, :128] / acc[:, 128:]).astype(bf16)
            for p4 in range(block_rows // ROWS):
                p = n * (block_rows // ROWS) + p4
                mine = out[ROWS * p4:ROWS * (p4 + 1), :]
                if b < 2:
                    o_ref[p, ROWS * b:ROWS * (b + 1), :] = mine
                else:
                    o_ref[p, 2 * ROWS:PACK, :] = mine[:PACK - 2 * ROWS]
                    tail = mine[PACK - 2 * ROWS:]
                    unused = lane_block(PIECE) == junk
                    for i in range(3):
                        rows = slice(PIECE * i, PIECE * (i + 1))
                        o_ref[p, rows, :] = jnp.where(unused, turned(tail, 32 * (3 - i)), o_ref[p, rows, :])


def attend(head, packed, labels):
    vmem = pl.BlockSpec(memory_space=pltpu.VMEM)
    return pl.pallas_call(
        attend_kernel,
        out_shape=jax.ShapeDtypeStruct((HEADS, PACK, 128), jnp.bfloat16),
        in_specs=[pl.BlockSpec(memory_space=pltpu.SMEM), vmem, vmem],
        out_specs=vmem,
        scratch_shapes=[
            pltpu.VMEM((KEYS, 128), jnp.bfloat16),
            pltpu.VMEM((KEYS, 128), jnp.bfloat16),
            pltpu.VMEM((KEYS, 256), jnp.bfloat16),
            pltpu.VMEM((ROWS, HEADS * 128), jnp.float32),
        ],
        cost_estimate=pl.CostEstimate(flops=3 * 4 * KEYS * KEYS * 128, bytes_accessed=3 * 10**6, transcendentals=3 * KEYS * KEYS),
        name="attend",
    )(head, packed, labels)


def project_kernel(x_ref, tokens_ref, weight_ref, o_ref, a_s):
    f32, bf16 = jnp.float32, jnp.bfloat16
    block = lane_block(PIECE)

    def turned(x, shift):
        return pltpu.roll(x.astype(f32), shift, 1).astype(bf16)

    def tail(h):
        first = (3 * h) % 4
        a, b, c = (turned(x_ref[h, PIECE * i:PIECE * (i + 1), :], 32 * (i + 1)) for i in range(3))
        return jnp.where(block == first, a, jnp.where(block == (first + 1) % 4, b, c))

    for g in range(HEADS // 4):
        for part in range(4):
            if part < 3:
                rows = [x_ref[4 * g + j, PIECE * part:PIECE * (part + 1), :] for j in range(4)]
            else:
                rows = [tail(4 * g + j) for j in range(4)]
            for i in range(3):
                a_s[PIECE * part:PIECE * (part + 1), 128 * (3 * g + i):128 * (3 * g + i + 1)] = jnp.where(
                    block < 3 - i, rows[i], rows[i + 1])
    for n in range(D // 512):
        cols = slice(512 * n, 512 * (n + 1))
        total = jnp.dot(a_s[...], weight_ref[:, cols], preferred_element_type=f32)
        for dst, src, count in SPANS:
            part = total[2 * dst:2 * (dst + count)].reshape(count, 2, 512)
            here = (slice(src, src + count), 0, slice(None), cols)
            o_ref[here] = (part + tokens_ref[here].astype(f32)).astype(bf16)


def project(returned, tokens, weight):
    vmem = pl.BlockSpec(memory_space=pltpu.VMEM)
    return pl.pallas_call(
        project_kernel,
        out_shape=jax.ShapeDtypeStruct(tokens.shape, jnp.bfloat16),
        in_specs=[vmem] * 3,
        out_specs=vmem,
        scratch_shapes=[pltpu.VMEM((BANDS * ROWS, D), jnp.bfloat16)],
        cost_estimate=pl.CostEstimate(flops=2 * 192 * D * D, bytes_accessed=7 * 10**6, transcendentals=0),
        name="project",
    )(returned, tokens, weight)


def per_device(qkv_grid, tokens, out_weight, regions):
    windows, members = lax.axis_size("win"), lax.axis_size("seq")
    half = members // 2
    groups = [
        [w * members + half + i for i in range(half)] + [(w + 1) % windows * members + i for i in range(half)]
        for w in range(windows)
    ]

    def exchange(x):
        return lax.all_to_all(x, ("win", "seq"), 0, 0, axis_index_groups=groups, tiled=True)

    seat = lax.axis_index("seq")
    labels = regions[:, 0].T
    western = lax.ppermute(labels, "win", [(w, (w + 1) % windows) for w in range(windows)])
    labels = jnp.where(seat < half, western, labels)
    head = lax.rem(seat + half, members).reshape(1)
    received = exchange(pack_qkv(qkv_grid))
    returned = exchange(attend(head, received, labels))
    return project(returned, tokens, out_weight)


def solution(mesh):
    in_specs = (P(None, "win", "seq", None), P(None, "win", "seq", None), P(), P(None, "win", None))
    out_specs = P(None, "win", "seq", None)
    return jax.shard_map(
        per_device, mesh=mesh, in_specs=in_specs, out_specs=out_specs, check_vma=False
    )
```

time: 174 us -> 110 us (0.63)
  the two profiles are of different devices: /device:TPU:112 before, /device:TPU:4 now
where the time goes in v1:
time: 110 us
  waiting for transfers between devices  34.4 us (31%)
  blocking collectives  30.9 us (28%)
  starting transfers between devices  26.3 us (24%)
  Pallas kernels  16.1 us (15%)
  local copies, waits for them, and re-layouts  1.25 us (1%)
    all_to_all x1, blocking collectives, exchange(): lax.all_to_all(x, ('win', 'seq'), 0, 0, axis_index_groups=groups, tiled=T...  30.9 us
    all_to_all x1, waiting for transfers between devices, exchange(): lax.all_to_all(x, ('win', 'seq'), 0, 0, axis_index_groups=groups, tiled=T...  25.9 us
    all_to_all x1, starting transfers between devices, exchange(): lax.all_to_all(x, ('win', 'seq'), 0, 0, axis_index_groups=groups, tiled=T...  24.4 us
    ppermute x1, waiting for transfers between devices, per_device(): lax.ppermute(labels, 'win', [(w, (w + 1) % windows) for w in range(window...  8.48 us
    pallas_call x1, Pallas kernels, attend(): pl.pallas_call(attend_kernel, out_shape=jax.ShapeDtypeStruct((HEADS, PACK...  7.53 us
    pallas_call x1, Pallas kernels, project(): pl.pallas_call(project_kernel, out_shape=jax.ShapeDtypeStruct(tokens.shap...  4.96 us
    pallas_call x1, Pallas kernels, pack_qkv(): pl.pallas_call(pack_in_kernel, out_shape=jax.ShapeDtypeStruct((HEADS, 3 *...  3.61 us
  transfers between devices with their start and end apart: 2, of which 2 were waited for; matrix products, arithmetic and copies ran while one was open for 1% of the time, Pallas kernels for 0%

profile of v1, /device:TPU:4, one launch (start us, length us, event | category | flops | bytes accessed | tf_op | source)
XLA Modules:
  0.0 109.6 jit_solution(8054570841628220358)
XLA Ops:
  0.0 3.6 %pack_qkv.1 = bf16[16,432,128]{2,1,0:T(8,128)(2,1)} custom-call(bf16[90,1,2,4608]{3,2,1,0:T(2,128)(2,1)} %x_ref.1), custom_call_target="tpu_custom_call" | custom-call | flops 10000000 | bytes 4000000 | tf_op jit(solution)/shard_map/pack_qkv/pallas_call | solution.py:68
  3.6 0.0 copy-start.1
  3.6 24.4 %all-to-all-start = ((bf16[16,432,128]{2,1,0:T(8,128)(2,1)}), bf16[16,432,128]{2,1,0:T(8,128)(2,1)S(1)}, u32[]{:S(2)}, u32[]{:S(2)}) async-start(bf16[16,432,128]{2,1,0:T(8,128)(2,1)} %pack_qkv.1), calls=%async_computation | async-start | bytes 3538944 | tf_op jit(solution)/shard_map/all_to_all | solution.py:216
  28.0 0.0 copy-done.1
  28.0 1.9 %collective-permute-start = (s32[32,90]{1,0:T(8,128)S(1)}, s32[32,90]{1,0:T(8,128)S(1)}, u32[]{:S(2)}, u32[]{:S(2)}) collective-permute-start(s32[32,90]{1,0:T(8,128)S(1)} %bitcast.5), channel_id=1, source_target_pairs={{0,16},{16,32},{32,48},{48,64},{64,80},{80,96},{96,112},{112,128},... | collective-permute-start | bytes 34568 | tf_op jit(solution)/shard_map/ppermute | solution.py:220
  30.0 8.5 %collective-permute-done = s32[32,90]{1,0:T(8,128)S(1)} collective-permute-done((s32[32,90]{1,0:T(8,128)S(1)}, s32[32,90]{1,0:T(8,128)S(1)}, u32[]{:S(2)}, u32[]{:S(2)}) %collective-permute-start) | collective-permute-done | bytes 11552 | tf_op jit(solution)/shard_map/ppermute | solution.py:220
  38.4 0.6 broadcast_select_fusion.labels_ref
  39.0 25.9 %all-to-all-done.x_ref = bf16[16,432,128]{2,1,0:T(8,128)(2,1)S(1)} async-done(((bf16[16,432,128]{2,1,0:T(8,128)(2,1)}), bf16[16,432,128]{2,1,0:T(8,128)(2,1)S(1)}, u32[]{:S(2)}, u32[]{:S(2)}) %all-to-all-start) | async-done | bytes 1769504 | tf_op jit(solution)/shard_map/all_to_all | solution.py:216
  65.0 0.0 copy-start
  65.0 1.2 %copy-done = bf16[16,432,128]{2,1,0:T(8,128)(2,1)} copy-done((bf16[16,432,128]{2,1,0:T(8,128)(2,1)}, bf16[16,432,128]{2,1,0:T(8,128)(2,1)S(1)}, u32[]{:S(2)}) %copy-start) | copy-done | bytes 1769496
  66.2 7.5 %attend.1 = bf16[16,144,128]{2,1,0:T(8,128)(2,1)} custom-call(s32[1]{0:T(128)} %bitcast.head_ref, bf16[16,432,128]{2,1,0:T(8,128)(2,1)} %copy-done, s32[32,90]{1,0:T(8,128)} %broadcast_select_fusion.labels_ref), custom_call_target="tpu_custom_call" | custom-call | flops 1610612736 | bytes 3000000 | tf_op jit(solution)/shard_map/attend/pallas_call | solution.py:148
  73.8 30.9 %all_to_all.10.x_ref = bf16[16,144,128]{2,1,0:T(8,128)(2,1)} all-to-all(bf16[16,144,128]{2,1,0:T(8,128)(2,1)} %attend.1), channel_id=1, replica_groups={{8,9,10,11,12,13,14,15,16,17,18,19,20,21,22,23},{24,25,26,27,28,29,30,3..., dimensions={0} | all-to-all | bytes 1179648 | tf_op jit(solution)/shard_map/all_to_all | solution.py:216
  104.6 5.0 %project.1 = bf16[90,1,2,1536]{3,2,1,0:T(2,128)(2,1)} custom-call(bf16[16,144,128]{2,1,0:T(8,128)(2,1)} %all_to_all.10.x_ref, bf16[90,1,2,1536]{3,2,1,0:T(2,128)(2,1)} %tokens_ref.1, bf16[1536,1536]{1,0:T(8,128)(2,1)} %weight_ref.1), custom_call_target="tpu_custom_call" | custom-call | flops 905969664 | bytes 7000000 | tf_op jit(solution)/shard_map/project/pallas_call | solution.py:196
Async XLA Ops:
  3.6 24.4 %copy-start.1 = (s32[90,1,32]{0,2,1:T(8,128)S(1)}, s32[90,1,32]{0,2,1:T(8,128)}, u32[]{:S(2)}) copy-start(s32[90,1,32]{0,2,1:T(8,128)} %param.7) | copy-start | bytes 34564
  3.6 61.4 %all-to-all-start = ((bf16[16,432,128]{2,1,0:T(8,128)(2,1)}), bf16[16,432,128]{2,1,0:T(8,128)(2,1)S(1)}, u32[]{:S(2)}, u32[]{:S(2)}) async-start(bf16[16,432,128]{2,1,0:T(8,128)(2,1)} %pack_qkv.1), calls=%async_computation | async-start | bytes 3538944 | tf_op jit(solution)/shard_map/all_to_all | solution.py:216
  28.0 10.4 %collective-permute-start = (s32[32,90]{1,0:T(8,128)S(1)}, s32[32,90]{1,0:T(8,128)S(1)}, u32[]{:S(2)}, u32[]{:S(2)}) collective-permute-start(s32[32,90]{1,0:T(8,128)S(1)} %bitcast.5), channel_id=1, source_target_pairs={{0,16},{16,32},{32,48},{48,64},{64,80},{80,96},{96,112},{112,128},... | collective-permute-start | bytes 34568 | tf_op jit(solution)/shard_map/ppermute | solution.py:220
  65.0 1.2 %copy-start = (bf16[16,432,128]{2,1,0:T(8,128)(2,1)}, bf16[16,432,128]{2,1,0:T(8,128)(2,1)S(1)}, u32[]{:S(2)}) copy-start(bf16[16,432,128]{2,1,0:T(8,128)(2,1)S(1)} %all-to-all-done.x_ref) | copy-start | bytes 5308420

commit v2 on v1

v2 whole, which is shorter than its diff:
```python
import jax
import jax.numpy as jnp
from jax import lax
from jax.experimental import pallas as pl
from jax.experimental.pallas import tpu as pltpu
from jax.sharding import PartitionSpec as P

D = 1536
HEADS = 16
HD = 96
WH = 30
WW = 32
BANDS = 3
ROWS = 64
TOKENS = 184
SENT = 416
TAIL = 136
PACK = 144
PIECE = 48
REST = 40
KEYS = HEADS * ROWS
HIDE = -1e30


def lane_block(rows):
    return lax.broadcasted_iota(jnp.int32, (rows, 128), 1) // 32


def head_lanes(load, h):
    g, j = divmod(h, 4)
    if j == 0:
        return load(3 * g)
    if j == 3:
        return load(3 * g + 2)
    first, second = load(3 * g + j - 1), load(3 * g + j)
    block = lane_block(first.shape[0])
    return jnp.where(block < 3 - j, second, first)


def turned(x, shift):
    return pltpu.roll(x.astype(jnp.float32), shift, 1).astype(jnp.bfloat16)


SPANS = ((0, 15, 30), (30, 75, 2), (32, 45, 30), (62, 77, 13), (75, 0, 15))
SEGMENTS = ((0, 136, 0, 0, 0, 0), (136, 184, 0, 136, 1, 0), (184, 272, 1, 0, 1, 48), (272, 368, 1, 88, 2, 0), (368, 408, 2, 0, 2, 96))


def pack_kernel(seat_ref, x_ref, labels_ref, o_ref, flat):
    f32, bf16 = jnp.float32, jnp.bfloat16
    flat[TOKENS - 8:, :] = jnp.zeros((flat.shape[0] - TOKENS + 8, 3 * D), bf16)
    for dst, src, count in SPANS:
        for r in range(0, count, 8):
            n = min(8, count - r)
            start = 2 * (dst + r)
            flat[start:start + 2 * n, :] = x_ref[src + r:src + r + n, 0].reshape(2 * n, 3 * D)
    row = lax.broadcasted_iota(jnp.int32, (8, WW), 0)
    column = lax.rem(2 * seat_ref[0] + jnp.where(row < 3, 0, WW // 2), WW)
    picks = (lax.broadcasted_iota(jnp.int32, (8, WW), 1) == column).astype(bf16)
    picked = jnp.dot(picks, labels_ref[...].astype(bf16), preferred_element_type=f32).astype(bf16)
    grid_row = lax.broadcasted_iota(jnp.int32, (90, 128), 0)
    lane = lax.broadcasted_iota(jnp.int32, (90, 128), 1) % 32
    band = lax.broadcasted_iota(jnp.int32, (8, 128), 0) % 3
    labels = jnp.zeros((8, 128), f32)
    for b in range(BANDS):
        place = ((grid_row == lane + WH * b) & (lane < WH)).astype(bf16)
        labels += jnp.where(band == b, jnp.dot(picked, place, preferred_element_type=f32), 0.0)
    labels = labels.astype(bf16)
    for h in range(HEADS):
        def rows(t, start, size):
            def load(tile):
                lanes = (12 * t + tile) * 128
                return flat[start:start + size, lanes:lanes + 128]
            return head_lanes(load, h)
        tail = rows(2, TOKENS - TAIL, TAIL)
        for start, end, t, first, section, skip in SEGMENTS:
            size = end - start
            moved = turned(tail[skip:skip + size], 32 * (3 - section))
            o_ref[h, start:end, :] = jnp.where(lane_block(size) == 3 - h % 4, moved, rows(t, first, size))
        o_ref[h, SENT - 8:, :] = jnp.where(lane_block(8) == 3 - h % 4, labels, rows(2, 40, 8))


def pack_qkv(seat, x, labels):
    vmem = pl.BlockSpec(memory_space=pltpu.VMEM)
    return pl.pallas_call(
        pack_kernel,
        out_shape=jax.ShapeDtypeStruct((HEADS, SENT, 128), jnp.bfloat16),
        in_specs=[pl.BlockSpec(memory_space=pltpu.SMEM), vmem, vmem],
        out_specs=vmem,
        scratch_shapes=[pltpu.VMEM((192, 3 * D), jnp.bfloat16)],
        cost_estimate=pl.CostEstimate(flops=10**7, bytes_accessed=4 * 10**6, transcendentals=0),
        compiler_params=pltpu.CompilerParams(vmem_limit_bytes=12 * 2**20),
        name="pack_qkv",
    )(seat, x, labels)


def attend_kernel(seat_ref, x_ref, o_ref, q_s, k_s, v_s, t_s, r_s):
    junk = 3 - lax.rem(seat_ref[0], 4)
    first = lax.rem(junk + 1, 4)
    second = lax.rem(junk + 2, 4)
    f32, bf16 = jnp.float32, jnp.bfloat16
    i32 = jnp.int32
    scale = HD ** -0.5 * 1.4426950408889634

    lane = lax.broadcasted_iota(i32, (ROWS, 128), 1) - 32 * junk
    inside = (lane >= 0) & (lane < 32)
    row = lax.broadcasted_iota(i32, (ROWS, 128), 0)
    sent_labels = jnp.concatenate([x_ref[p, SENT - 8:, :] for p in range(HEADS // 2)], 0)
    pick_row = lax.broadcasted_iota(i32, (ROWS, HEADS * 128), 0)
    pick_source = lax.broadcasted_iota(i32, (ROWS, HEADS * 128), 1) // 128
    pick_base = 8 * (pick_source % 8) + 3 * (pick_source // 8)
    tail_block = lane_block(TAIL)
    rest_block = lane_block(REST)
    eight = lax.broadcasted_iota(i32, (8, 128), 0)

    def block_of(load, b):
        if b < 2:
            return load(ROWS * b, ROWS)
        last = jnp.where(eight < 4, load(TOKENS - 8, 8), load(56, 8))
        return jnp.concatenate([load(120, 56), last], 0)

    for b in range(BANDS):
        token = jnp.where(row < 60, row, row - 60) if b == 2 else row
        spare = (row < 4) if b == 2 else (row >= 60)
        grows = (inside & (lane == token // 2)).astype(bf16)
        by_source = lax.dot_general(
            grows, sent_labels, (((1,), (1,)), ((), ())), preferred_element_type=f32).astype(bf16)
        picks = (pick_row == pick_base + b).astype(bf16)
        r_s[...] = jnp.dot(by_source, picks, preferred_element_type=f32)
        for p in range(HEADS):
            label = jnp.where(spare, 3, r_s[:, 128 * p:128 * (p + 1)].astype(i32))
            same = label == lane
            q = block_of(lambda start, size: x_ref[p, start:start + size, :], b)
            k = block_of(lambda start, size: x_ref[p, TOKENS + start:TOKENS + start + size, :], b)
            here = slice(ROWS * p, ROWS * (p + 1))
            q_s[here, :] = jnp.where(inside, jnp.where(same, 1.0, 0.0).astype(bf16), q)
            k_s[here, :] = jnp.where(inside, jnp.where(same, 0.0, HIDE).astype(bf16), k)
            if b == 0:
                x, y, z = (turned(x_ref[p, TAIL * i:TAIL * (i + 1), :], 32 * (i + 1)) for i in range(3))
                t_s[p, :TOKENS - TAIL, :] = x_ref[p, 2 * TOKENS:3 * TOKENS - TAIL, :]
                t_s[p, TOKENS - TAIL:, :] = jnp.where(tail_block == first, x, jnp.where(tail_block == second, y, z))
            v_s[here, :128] = block_of(lambda start, size: t_s[p, start:start + size, :], b)
        if b == 0:
            v_s[:, 128:] = jnp.ones((KEYS, 128), bf16)
        block_rows = 256
        for n in range(KEYS // block_rows):
            q = q_s[block_rows * n:block_rows * (n + 1), :]
            s = lax.dot_general(q, k_s[...], (((1,), (1,)), ((), ())), preferred_element_type=f32)
            m = jnp.max(s, axis=1, keepdims=True)
            weights = jnp.exp2((s - m) * scale).astype(bf16)
            acc = jnp.dot(weights, v_s[...], preferred_element_type=f32)
            out = (acc[:, :128] / acc[:, 128:]).astype(bf16)
            for i in range(block_rows // ROWS):
                p = n * (block_rows // ROWS) + i
                mine = out[ROWS * i:ROWS * (i + 1), :]
                if b < 2:
                    o_ref[p, ROWS * b:ROWS * (b + 1), :] = mine
                else:
                    o_ref[p, 56:64, :] = jnp.where(eight < 4, o_ref[p, 56:64, :], mine[56:])
                    o_ref[p, 120:128, :] = jnp.where(eight < 4, o_ref[p, 120:128, :], mine[:8])
                    o_ref[p, 128:PACK, :] = mine[8:24]
                    rest = mine[24:]
                    for k in range(3):
                        rows = slice(PIECE * k, PIECE * k + REST)
                        o_ref[p, rows, :] = jnp.where(rest_block == junk, turned(rest, 32 * (3 - k)), o_ref[p, rows, :])


def attend(seat, packed):
    return pl.pallas_call(
        attend_kernel,
        out_shape=jax.ShapeDtypeStruct((HEADS, PACK, 128), jnp.bfloat16),
        in_specs=[pl.BlockSpec(memory_space=pltpu.SMEM), pl.BlockSpec(memory_space=pltpu.VMEM)],
        out_specs=pl.BlockSpec(memory_space=pltpu.VMEM),
        scratch_shapes=[
            pltpu.VMEM((KEYS, 128), jnp.bfloat16),
            pltpu.VMEM((KEYS, 128), jnp.bfloat16),
            pltpu.VMEM((KEYS, 256), jnp.bfloat16),
            pltpu.VMEM((HEADS, TOKENS, 128), jnp.bfloat16),
            pltpu.VMEM((ROWS, HEADS * 128), jnp.float32),
        ],
        cost_estimate=pl.CostEstimate(flops=3 * 4 * KEYS * KEYS * 128, bytes_accessed=3 * 10**6, transcendentals=3 * KEYS * KEYS),
        compiler_params=pltpu.CompilerParams(vmem_limit_bytes=16 * 2**20),
        name="attend",
    )(seat, packed)


def project_kernel(x_ref, tokens_ref, weight_ref, o_ref, a_s):
    f32, bf16 = jnp.float32, jnp.bfloat16
    rest_block = lane_block(REST)

    def rest(h):
        first = (3 * h) % 4
        a, b, c = (turned(x_ref[h, PIECE * i:PIECE * i + REST, :], 32 * (i + 1)) for i in range(3))
        return jnp.where(rest_block == first, a, jnp.where(rest_block == (first + 1) % 4, b, c))

    a_s[TOKENS:, :] = jnp.zeros((a_s.shape[0] - TOKENS, D), bf16)
    for g in range(HEADS // 4):
        for part in range(4):
            size = PIECE if part < 3 else REST
            if part < 3:
                rows = [x_ref[4 * g + j, PIECE * part:PIECE * (part + 1), :] for j in range(4)]
            else:
                rows = [rest(4 * g + j) for j in range(4)]
            for i in range(3):
                lanes = slice(128 * (3 * g + i), 128 * (3 * g + i + 1))
                a_s[PIECE * part:PIECE * part + size, lanes] = jnp.where(
                    lane_block(size) < 3 - i, rows[i], rows[i + 1])
    for n in range(D // 512):
        cols = slice(512 * n, 512 * (n + 1))
        total = jnp.dot(a_s[...], weight_ref[:, cols], preferred_element_type=f32)
        for dst, src, count in SPANS:
            part = total[2 * dst:2 * (dst + count)].reshape(count, 2, 512)
            here = (slice(src, src + count), 0, slice(None), cols)
            o_ref[here] = (part + tokens_ref[here].astype(f32)).astype(bf16)


def project(returned, tokens, weight):
    vmem = pl.BlockSpec(memory_space=pltpu.VMEM)
    return pl.pallas_call(
        project_kernel,
        out_shape=jax.ShapeDtypeStruct(tokens.shape, jnp.bfloat16),
        in_specs=[vmem] * 3,
        out_specs=vmem,
        scratch_shapes=[pltpu.VMEM((192, D), jnp.bfloat16)],
        cost_estimate=pl.CostEstimate(flops=2 * 192 * D * D, bytes_accessed=7 * 10**6, transcendentals=0),
        compiler_params=pltpu.CompilerParams(vmem_limit_bytes=12 * 2**20),
        name="project",
    )(returned, tokens, weight)


def per_device(qkv_grid, tokens, out_weight, regions):
    windows, members = lax.axis_size("win"), lax.axis_size("seq")
    half = members // 2
    groups = [
        [w * members + half + i for i in range(half)] + [(w + 1) % windows * members + i for i in range(half)]
        for w in range(windows)
    ]

    def exchange(x):
        return lax.all_to_all(x, ("win", "seq"), 0, 0, axis_index_groups=groups, tiled=True)

    seat = lax.rem(lax.axis_index("seq") + half, members).reshape(1)
    received = exchange(pack_qkv(seat, qkv_grid, regions[:, 0].T))
    returned = exchange(attend(seat, received))
    return project(returned, tokens, out_weight)


def solution(mesh):
    in_specs = (P(None, "win", "seq", None), P(None, "win", "seq", None), P(), P(None, "win", None))
    out_specs = P(None, "win", "seq", None)
    return jax.shard_map(
        per_device, mesh=mesh, in_specs=in_specs, out_specs=out_specs, check_vma=False
    )
```

time: 110 us -> 98.5 us (0.90)
  blocking collectives: 30.9 us -> 87.3 us
  waiting for transfers between devices: 34.4 us -> 0 us
  starting transfers between devices: 26.3 us -> 0 us
  Pallas kernels: 16.1 us -> 8.84 us
    all_to_all x1 -> x2, blocking collectives: 30.9 us -> 87.3 us  [exchange(): lax.all_to_all(x, ('win', 'seq'), 0, 0, axis_index_groups=groups, tiled=T...]
    all_to_all x1 -> x0, waiting for transfers between devices: 25.9 us -> none  [exchange(): lax.all_to_all(x, ('win', 'seq'), 0, 0, axis_index_groups=groups, tiled=T...]
    all_to_all x1 -> x0, starting transfers between devices: 24.4 us -> none  [exchange(): lax.all_to_all(x, ('win', 'seq'), 0, 0, axis_index_groups=groups, tiled=T...]
    ppermute x1 -> x0, waiting for transfers between devices: 8.48 us -> none  [per_device(): lax.ppermute(labels, 'win', [(w, (w + 1) % windows) for w in range(window...]
    pallas_call x1, Pallas kernels: 3.61 us -> 0.93 us  [pack_qkv(): pl.pallas_call(pack_kernel, out_shape=jax.ShapeDtypeStruct((HEADS, SENT,...]
    pallas_call x1, Pallas kernels: 4.96 us -> 2.29 us  [project(): pl.pallas_call(project_kernel, out_shape=jax.ShapeDtypeStruct(tokens.shap...]
    ppermute x1 -> x0, starting transfers between devices: 1.92 us -> none  [per_device(): lax.ppermute(labels, 'win', [(w, (w + 1) % windows) for w in range(window...]
    pallas_call x1, Pallas kernels: 7.53 us -> 5.62 us  [attend(): pl.pallas_call(attend_kernel, out_shape=jax.ShapeDtypeStruct((HEADS, PACK...]
  transfers between devices with their start and end apart: 2 -> 0, of which waited for: 2 -> 0; matrix products, arithmetic and copies ran while one was open for 1% -> 0% of each run, Pallas kernels for 0% -> 0%
where the time goes in v2:
time: 98.5 us; the launch traced here: 98.3 us
  blocking collectives  87.3 us (89%)
  Pallas kernels  8.84 us (9%)
  local copies, waits for them, and re-layouts  2.16 us (2%)
    all_to_all x2, blocking collectives, exchange(): lax.all_to_all(x, ('win', 'seq'), 0, 0, axis_index_groups=groups, tiled=T...  87.3 us
    pallas_call x1, Pallas kernels, attend(): pl.pallas_call(attend_kernel, out_shape=jax.ShapeDtypeStruct((HEADS, PACK...  5.62 us
    pallas_call x1, Pallas kernels, project(): pl.pallas_call(project_kernel, out_shape=jax.ShapeDtypeStruct(tokens.shap...  2.29 us
    unnamed x8, local copies, waits for them, and re-layouts  2.16 us

profile of v2, /device:TPU:4, one launch (start us, length us, event | category | flops | bytes accessed | tf_op | source)
XLA Modules:
  0.0 98.3 jit_solution(12404216368343668153)
XLA Ops:
  0.0 0.0 copy-start.1
  0.0 1.4 %copy-done.1 = bf16[90,1,2,4608]{3,2,1,0:T(2,128)(2,1)S(1)} copy-done((bf16[90,1,2,4608]{3,2,1,0:T(2,128)(2,1)S(1)}, bf16[90,1,2,4608]{3,2,1,0:T(2,128)(2,1)}, u32[]{:S(2)}) %copy-start.1) | copy-done | bytes 1658904
  1.4 0.0 copy-start.3
  1.4 0.7 copy-done.3
  2.2 0.9 pack_qkv.1
  3.1 63.4 %all_to_all.10.x_ref = bf16[16,416,128]{2,1,0:T(8,128)(2,1)S(1)} all-to-all(bf16[16,416,128]{2,1,0:T(8,128)(2,1)S(1)} %pack_qkv.1), channel_id=1, replica_groups={{8,9,10,11,12,13,14,15,16,17,18,19,20,21,22,23},{24,25,26,27,28,29,30,3..., dimensions={0} | all-to-all | bytes 3407872 | tf_op jit(solution)/shard_map/all_to_all | solution.py:239
  66.5 0.0 copy-start
  66.5 0.0 copy-start.2
  66.5 5.6 %attend.1 = bf16[16,144,128]{2,1,0:T(8,128)(2,1)S(1)} custom-call(s32[1]{0:T(128)} %bitcast.seat_ref, bf16[16,416,128]{2,1,0:T(8,128)(2,1)S(1)} %all_to_all.10.x_ref), custom_call_target="tpu_custom_call" | custom-call | flops 1610612736 | bytes 3000000 | tf_op jit(solution)/shard_map/attend/pallas_call | solution.py:168
  72.2 23.8 %all_to_all.11.x_ref = bf16[16,144,128]{2,1,0:T(8,128)(2,1)S(1)} all-to-all(bf16[16,144,128]{2,1,0:T(8,128)(2,1)S(1)} %attend.1), channel_id=1, replica_groups={{8,9,10,11,12,13,14,15,16,17,18,19,20,21,22,23},{24,25,26,27,28,29,30,3..., dimensions={0} | all-to-all | bytes 1179648 | tf_op jit(solution)/shard_map/all_to_all | solution.py:239
  96.0 0.0 copy-done
  96.0 0.0 copy-done.2
  96.0 2.3 %project.1 = bf16[90,1,2,1536]{3,2,1,0:T(2,128)(2,1)} custom-call(bf16[16,144,128]{2,1,0:T(8,128)(2,1)S(1)} %all_to_all.11.x_ref, bf16[90,1,2,1536]{3,2,1,0:T(2,128)(2,1)S(1)} %copy-done.2, bf16[1536,1536]{1,0:T(8,128)(2,1)S(1)} %copy-done), custom_call_target="tpu_custom_call" | custom-call | flops 905969664 | bytes 7000000 | tf_op jit(solution)/shard_map/project/pallas_call | solution.py:218
Async XLA Ops:
  0.0 1.4 %copy-start.1 = (bf16[90,1,2,4608]{3,2,1,0:T(2,128)(2,1)S(1)}, bf16[90,1,2,4608]{3,2,1,0:T(2,128)(2,1)}, u32[]{:S(2)}) copy-start(bf16[90,1,2,4608]{3,2,1,0:T(2,128)(2,1)} %x_ref.1) | copy-start | bytes 4976644
  1.4 0.7 copy-start.3
  66.5 29.5 %copy-start = (bf16[1536,1536]{1,0:T(8,128)(2,1)S(1)}, bf16[1536,1536]{1,0:T(8,128)(2,1)}, u32[]{:S(2)}) copy-start(bf16[1536,1536]{1,0:T(8,128)(2,1)} %weight_ref.1) | copy-start | bytes 14155780
  66.5 29.5 %copy-start.2 = (bf16[90,1,2,1536]{3,2,1,0:T(2,128)(2,1)S(1)}, bf16[90,1,2,1536]{3,2,1,0:T(2,128)(2,1)}, u32[]{:S(2)}) copy-start(bf16[90,1,2,1536]{3,2,1,0:T(2,128)(2,1)} %tokens_ref.1) | copy-start | bytes 1658884

commit v3 on v2

--- a/solution.py
+++ b/solution.py
@@ -15,9 +15,8 @@
 TOKENS = 184
 SENT = 416
 TAIL = 136
-PACK = 144
-PIECE = 48
-REST = 40
+PACK = 136
+REST = 44
 KEYS = HEADS * ROWS
 HIDE = -1e30
 
@@ -56,7 +55,7 @@
     row = lax.broadcasted_iota(jnp.int32, (8, WW), 0)
     column = lax.rem(2 * seat_ref[0] + jnp.where(row < 3, 0, WW // 2), WW)
     picks = (lax.broadcasted_iota(jnp.int32, (8, WW), 1) == column).astype(bf16)
-    picked = jnp.dot(picks, labels_ref[...].astype(bf16), preferred_element_type=f32).astype(bf16)
+    picked = jnp.dot(picks, labels_ref[...], preferred_element_type=f32).astype(bf16)
     grid_row = lax.broadcasted_iota(jnp.int32, (90, 128), 0)
     lane = lax.broadcasted_iota(jnp.int32, (90, 128), 1) % 32
     band = lax.broadcasted_iota(jnp.int32, (8, 128), 0) % 3
@@ -118,36 +117,46 @@
         last = jnp.where(eight < 4, load(TOKENS - 8, 8), load(56, 8))
         return jnp.concatenate([load(120, 56), last], 0)
 
-    for b in range(BANDS):
+    def prepare(b):
         token = jnp.where(row < 60, row, row - 60) if b == 2 else row
-        spare = (row < 4) if b == 2 else (row >= 60)
         grows = (inside & (lane == token // 2)).astype(bf16)
         by_source = lax.dot_general(
             grows, sent_labels, (((1,), (1,)), ((), ())), preferred_element_type=f32).astype(bf16)
         picks = (pick_row == pick_base + b).astype(bf16)
-        r_s[...] = jnp.dot(by_source, picks, preferred_element_type=f32)
-        for p in range(HEADS):
-            label = jnp.where(spare, 3, r_s[:, 128 * p:128 * (p + 1)].astype(i32))
-            same = label == lane
-            q = block_of(lambda start, size: x_ref[p, start:start + size, :], b)
-            k = block_of(lambda start, size: x_ref[p, TOKENS + start:TOKENS + start + size, :], b)
-            here = slice(ROWS * p, ROWS * (p + 1))
-            q_s[here, :] = jnp.where(inside, jnp.where(same, 1.0, 0.0).astype(bf16), q)
-            k_s[here, :] = jnp.where(inside, jnp.where(same, 0.0, HIDE).astype(bf16), k)
-            if b == 0:
-                x, y, z = (turned(x_ref[p, TAIL * i:TAIL * (i + 1), :], 32 * (i + 1)) for i in range(3))
-                t_s[p, :TOKENS - TAIL, :] = x_ref[p, 2 * TOKENS:3 * TOKENS - TAIL, :]
-                t_s[p, TOKENS - TAIL:, :] = jnp.where(tail_block == first, x, jnp.where(tail_block == second, y, z))
-            v_s[here, :128] = block_of(lambda start, size: t_s[p, start:start + size, :], b)
+        r_s[b % 2] = jnp.dot(by_source, picks, preferred_element_type=f32)
+
+    def unpack(b, p):
+        spare = (row < 4) if b == 2 else (row >= 60)
+        label = jnp.where(spare, 3, r_s[b % 2, :, 128 * p:128 * (p + 1)].astype(i32))
+        same = label == lane
+        q = block_of(lambda start, size: x_ref[p, start:start + size, :], b)
+        k = block_of(lambda start, size: x_ref[p, TOKENS + start:TOKENS + start + size, :], b)
+        here = slice(ROWS * p, ROWS * (p + 1))
+        q_s[b % 2, here, :] = jnp.where(inside, jnp.where(same, 1.0, 0.0).astype(bf16), q)
+        k_s[b % 2, here, :] = jnp.where(inside, jnp.where(same, 0.0, HIDE).astype(bf16), k)
         if b == 0:
-            v_s[:, 128:] = jnp.ones((KEYS, 128), bf16)
+            x, y, z = (turned(x_ref[p, TAIL * i:TAIL * (i + 1), :], 32 * (i + 1)) for i in range(3))
+            t_s[p, :TOKENS - TAIL, :] = x_ref[p, 2 * TOKENS:3 * TOKENS - TAIL, :]
+            t_s[p, TOKENS - TAIL:, :] = jnp.where(tail_block == first, x, jnp.where(tail_block == second, y, z))
+        v_s[b % 2, here, :128] = block_of(lambda start, size: t_s[p, start:start + size, :], b)
+
+    v_s[:, :, 128:] = jnp.ones((2, KEYS, 128), bf16)
+    prepare(0)
+    for p in range(HEADS):
+        unpack(0, p)
+    for b in range(BANDS):
+        if b + 1 < BANDS:
+            prepare(b + 1)
         block_rows = 256
         for n in range(KEYS // block_rows):
-            q = q_s[block_rows * n:block_rows * (n + 1), :]
-            s = lax.dot_general(q, k_s[...], (((1,), (1,)), ((), ())), preferred_element_type=f32)
+            q = q_s[b % 2, block_rows * n:block_rows * (n + 1), :]
+            s = lax.dot_general(q, k_s[b % 2], (((1,), (1,)), ((), ())), preferred_element_type=f32)
+            if b + 1 < BANDS:
+                for p in range(4 * n, 4 * n + 4):
+                    unpack(b + 1, p)
             m = jnp.max(s, axis=1, keepdims=True)
             weights = jnp.exp2((s - m) * scale).astype(bf16)
-            acc = jnp.dot(weights, v_s[...], preferred_element_type=f32)
+            acc = jnp.dot(weights, v_s[b % 2], preferred_element_type=f32)
             out = (acc[:, :128] / acc[:, 128:]).astype(bf16)
             for i in range(block_rows // ROWS):
                 p = n * (block_rows // ROWS) + i
@@ -157,10 +166,10 @@
                 else:
                     o_ref[p, 56:64, :] = jnp.where(eight < 4, o_ref[p, 56:64, :], mine[56:])
                     o_ref[p, 120:128, :] = jnp.where(eight < 4, o_ref[p, 120:128, :], mine[:8])
-                    o_ref[p, 128:PACK, :] = mine[8:24]
-                    rest = mine[24:]
+                    o_ref[p, 128:PACK, :] = mine[8:16]
+                    rest = mine[16:60]
                     for k in range(3):
-                        rows = slice(PIECE * k, PIECE * k + REST)
+                        rows = slice(REST * k, REST * (k + 1))
                         o_ref[p, rows, :] = jnp.where(rest_block == junk, turned(rest, 32 * (3 - k)), o_ref[p, rows, :])
 
 
@@ -171,11 +180,11 @@
         in_specs=[pl.BlockSpec(memory_space=pltpu.SMEM), pl.BlockSpec(memory_space=pltpu.VMEM)],
         out_specs=pl.BlockSpec(memory_space=pltpu.VMEM),
         scratch_shapes=[
-            pltpu.VMEM((KEYS, 128), jnp.bfloat16),
-            pltpu.VMEM((KEYS, 128), jnp.bfloat16),
-            pltpu.VMEM((KEYS, 256), jnp.bfloat16),
+            pltpu.VMEM((2, KEYS, 128), jnp.bfloat16),
+            pltpu.VMEM((2, KEYS, 128), jnp.bfloat16),
+            pltpu.VMEM((2, KEYS, 256), jnp.bfloat16),
             pltpu.VMEM((HEADS, TOKENS, 128), jnp.bfloat16),
-            pltpu.VMEM((ROWS, HEADS * 128), jnp.float32),
+            pltpu.VMEM((2, ROWS, HEADS * 128), jnp.float32),
         ],
         cost_estimate=pl.CostEstimate(flops=3 * 4 * KEYS * KEYS * 128, bytes_accessed=3 * 10**6, transcendentals=3 * KEYS * KEYS),
         compiler_params=pltpu.CompilerParams(vmem_limit_bytes=16 * 2**20),
@@ -189,21 +198,19 @@
 
     def rest(h):
         first = (3 * h) % 4
-        a, b, c = (turned(x_ref[h, PIECE * i:PIECE * i + REST, :], 32 * (i + 1)) for i in range(3))
+        a, b, c = (turned(x_ref[h, REST * i:REST * (i + 1), :], 32 * (i + 1)) for i in range(3))
         return jnp.where(rest_block == first, a, jnp.where(rest_block == (first + 1) % 4, b, c))
 
-    a_s[TOKENS:, :] = jnp.zeros((a_s.shape[0] - TOKENS, D), bf16)
+    a_s[176:, :] = jnp.zeros((a_s.shape[0] - 176, D), bf16)
     for g in range(HEADS // 4):
-        for part in range(4):
-            size = PIECE if part < 3 else REST
-            if part < 3:
-                rows = [x_ref[4 * g + j, PIECE * part:PIECE * (part + 1), :] for j in range(4)]
+        for start, end in ((0, 48), (48, 96), (96, PACK), (PACK, PACK + REST)):
+            if start < PACK:
+                rows = [x_ref[4 * g + j, start:end, :] for j in range(4)]
             else:
                 rows = [rest(4 * g + j) for j in range(4)]
             for i in range(3):
                 lanes = slice(128 * (3 * g + i), 128 * (3 * g + i + 1))
-                a_s[PIECE * part:PIECE * part + size, lanes] = jnp.where(
-                    lane_block(size) < 3 - i, rows[i], rows[i + 1])
+                a_s[start:end, lanes] = jnp.where(lane_block(end - start) < 3 - i, rows[i], rows[i + 1])
     for n in range(D // 512):
         cols = slice(512 * n, 512 * (n + 1))
         total = jnp.dot(a_s[...], weight_ref[:, cols], preferred_element_type=f32)
@@ -239,7 +246,7 @@
         return lax.all_to_all(x, ("win", "seq"), 0, 0, axis_index_groups=groups, tiled=True)
 
     seat = lax.rem(lax.axis_index("seq") + half, members).reshape(1)
-    received = exchange(pack_qkv(seat, qkv_grid, regions[:, 0].T))
+    received = exchange(pack_qkv(seat, qkv_grid, regions[:, 0].T.astype(jnp.bfloat16)))
     returned = exchange(attend(seat, received))
     return project(returned, tokens, out_weight)
 

time: 98.5 us -> 97.4 us (0.989)
    unnamed x8 -> x6, local copies, waits for them, and re-layouts: 2.16 us -> 1.44 us
where the time goes in v3:
time: 97.4 us; the launch traced here: 97.2 us
  blocking collectives  86.6 us (89%)
  Pallas kernels  8.4 us (9%)
  local copies, waits for them, and re-layouts  1.44 us (1%)
    all_to_all x2, blocking collectives, exchange(): lax.all_to_all(x, ('win', 'seq'), 0, 0, axis_index_groups=groups, tiled=T...  86.6 us
    pallas_call x1, Pallas kernels, attend(): pl.pallas_call(attend_kernel, out_shape=jax.ShapeDtypeStruct((HEADS, PACK...  5.15 us
    pallas_call x1, Pallas kernels, project(): pl.pallas_call(project_kernel, out_shape=jax.ShapeDtypeStruct(tokens.shap...  2.32 us

profile of v3, /device:TPU:4, one launch (start us, length us, event | category | flops | bytes accessed | tf_op | source)
XLA Modules:
  0.0 97.2 jit_solution(7716479611580309887)
XLA Ops:
  0.0 0.7 convert_bitcast_fusion.labels_ref
  0.7 0.0 copy-start.1
  0.7 1.4 %copy-done.1 = bf16[90,1,2,4608]{3,2,1,0:T(2,128)(2,1)S(1)} copy-done((bf16[90,1,2,4608]{3,2,1,0:T(2,128)(2,1)S(1)}, bf16[90,1,2,4608]{3,2,1,0:T(2,128)(2,1)}, u32[]{:S(2)}) %copy-start.1) | copy-done | bytes 1658904
  2.2 0.9 pack_qkv.1
  3.1 63.4 %all_to_all.10.x_ref = bf16[16,416,128]{2,1,0:T(8,128)(2,1)S(1)} all-to-all(bf16[16,416,128]{2,1,0:T(8,128)(2,1)S(1)} %pack_qkv.1), channel_id=1, replica_groups={{8,9,10,11,12,13,14,15,16,17,18,19,20,21,22,23},{24,25,26,27,28,29,30,3..., dimensions={0} | all-to-all | bytes 3407872 | tf_op jit(solution)/shard_map/all_to_all | solution.py:246
  66.5 0.0 copy-start
  66.5 0.0 copy-start.2
  66.5 5.2 %attend.1 = bf16[16,136,128]{2,1,0:T(8,128)(2,1)S(1)} custom-call(s32[1]{0:T(128)} %bitcast.seat_ref, bf16[16,416,128]{2,1,0:T(8,128)(2,1)S(1)} %all_to_all.10.x_ref), custom_call_target="tpu_custom_call" | custom-call | flops 1610612736 | bytes 3000000 | tf_op jit(solution)/shard_map/attend/pallas_call | solution.py:177
  71.7 23.1 %all_to_all.11.x_ref = bf16[16,136,128]{2,1,0:T(8,128)(2,1)S(1)} all-to-all(bf16[16,136,128]{2,1,0:T(8,128)(2,1)S(1)} %attend.1), channel_id=1, replica_groups={{8,9,10,11,12,13,14,15,16,17,18,19,20,21,22,23},{24,25,26,27,28,29,30,3..., dimensions={0} | all-to-all | bytes 1114112 | tf_op jit(solution)/shard_map/all_to_all | solution.py:246
  94.8 0.0 copy-done
  94.8 0.0 copy-done.2
  94.8 2.3 %project.1 = bf16[90,1,2,1536]{3,2,1,0:T(2,128)(2,1)} custom-call(bf16[16,136,128]{2,1,0:T(8,128)(2,1)S(1)} %all_to_all.11.x_ref, bf16[90,1,2,1536]{3,2,1,0:T(2,128)(2,1)S(1)} %copy-done.2, bf16[1536,1536]{1,0:T(8,128)(2,1)S(1)} %copy-done), custom_call_target="tpu_custom_call" | custom-call | flops 905969664 | bytes 7000000 | tf_op jit(solution)/shard_map/project/pallas_call | solution.py:225
Async XLA Ops:
  0.7 1.4 %copy-start.1 = (bf16[90,1,2,4608]{3,2,1,0:T(2,128)(2,1)S(1)}, bf16[90,1,2,4608]{3,2,1,0:T(2,128)(2,1)}, u32[]{:S(2)}) copy-start(bf16[90,1,2,4608]{3,2,1,0:T(2,128)(2,1)} %x_ref.1) | copy-start | bytes 4976644
  66.5 28.3 %copy-start = (bf16[1536,1536]{1,0:T(8,128)(2,1)S(1)}, bf16[1536,1536]{1,0:T(8,128)(2,1)}, u32[]{:S(2)}) copy-start(bf16[1536,1536]{1,0:T(8,128)(2,1)} %weight_ref.1) | copy-start | bytes 14155780
  66.5 28.3 %copy-start.2 = (bf16[90,1,2,1536]{3,2,1,0:T(2,128)(2,1)S(1)}, bf16[90,1,2,1536]{3,2,1,0:T(2,128)(2,1)}, u32[]{:S(2)}) copy-start(bf16[90,1,2,1536]{3,2,1,0:T(2,128)(2,1)} %tokens_ref.1) | copy-start | bytes 1658884
